TPU v7x, 32 devices: a whole 2x2x4 slice. The times are simulated.
32 devices in a mesh: section: 2 (over core), seq: 4 (over y, x), head: 4 (over z).
Axes of the slice: x: 2, y: 2, z: 4, core: 2. Of those that a mesh axis runs over, the one named last changes fastest.
Arguments:
- x_in: bfloat16 [2, 1024, 8192], P('section', 'seq', 'head'), may hold values from -6 to 6
- b_in: bfloat16 [2, 1024, 2048], P('section', 'seq', 'head'), may hold values from -6 to 6
- c_in: bfloat16 [2, 1024, 2048], P('section', 'seq', 'head'), may hold values from -6 to 6
- z_in: bfloat16 [2, 1024, 8192], P('section', 'seq', 'head'), may hold values from -6 to 6
- dt_raw: float32 [2, 128, 1024], P('section', 'head', 'seq'), may hold values from -5 to 5
- conv_x: float32 [2, 4, 8192], P('section', None, 'head'), may hold values from -3 to 3
- conv_b: float32 [2, 4, 2048], P('section', None, 'head'), may hold values from -3 to 3
- conv_c: float32 [2, 4, 2048], P('section', None, 'head'), may hold values from -3 to 3
- a_rate: float32 [2, 128], P('section', 'head'), may hold values from 0.0001 to 1
- dt_bias: float32 [2, 128], P('section', 'head'), may hold values from -3 to -0.5
- skip_d: float32 [2, 128], P('section', 'head'), may hold values from 0.5 to 2
- norm_gain: float32 [2, 8192], P('section', 'head'), may hold values from 0.25 to 1.75
- out_weight: bfloat16 [2, 8192, 8192], P('section', 'head', 'seq'), may hold values from -0.0625 to 0.0625
Outputs:
- mixed: bfloat16 [2, 1024, 8192], P('section', ('seq', 'head'))
All inputs are finite; a program needn't handle non-finite values.
Results may differ from a plain program's by a relative error of at most 0.007.
Values may be sent and summed in bfloat16 or wider, within the bound.
A program may use at most 128 MiB of HBM per device.

v0:
```python
import functools
import math

import jax
import jax.numpy as jnp
from jax import lax
from jax.experimental import pallas as pl
from jax.experimental.pallas import tpu as pltpu
from jax.sharding import PartitionSpec as P

N = 256


epsilon = 1e-05


def passed_along(block, axis, distance):
    devices = range(lax.axis_size(axis))
    route = [(i - distance, i) for i in devices if i - distance in devices]
    return lax.ppermute(block, axis, route)


def carry_kernel(shards, decay, block, carried, inbox, outbox, send, recv):
    me = lax.axis_index("seq")
    chunks = block.shape[0]
    after, before = lax.rem(me + 1, shards), lax.rem(me + shards - 1, shards)
    barrier = pltpu.get_barrier_semaphore()
    for neighbour in (before, after):
        pl.semaphore_signal(barrier, inc=1, device_id={"seq": neighbour})
    pl.semaphore_wait(barrier, 2)

    def hand_on(c):
        return pltpu.make_async_remote_copy(
            outbox.at[c], inbox.at[c], send.at[c], recv.at[c], device_id={"seq": after}
        )

    for c in range(chunks):

        @pl.when(me == 0)
        def _():
            carried[c] = jnp.zeros(carried.shape[1:], carried.dtype)

        @pl.when(me > 0)
        def _():
            hand_on(c).wait_recv()
            carried[c] = inbox[c]

        @pl.when(me < shards - 1)
        def _():
            new = decay[c] * carried[c].astype(jnp.float32) + block[c]
            outbox[c] = new.astype(jnp.bfloat16)
            hand_on(c).start()

    for c in range(chunks):

        @pl.when(me < shards - 1)
        def _():
            hand_on(c).wait_send()


def entering(decay, block, shards):
    heads, p, n = block.shape
    chunks = math.gcd(8, heads)
    shape = (chunks, heads // chunks, p, n)
    spread = jnp.broadcast_to(decay.reshape(chunks, -1, 1, 1), (chunks, heads // chunks, 1, n))
    bf16 = jnp.bfloat16
    dma = pltpu.SemaphoreType.DMA
    carried = pl.pallas_call(
        functools.partial(carry_kernel, shards),
        out_shape=jax.ShapeDtypeStruct(shape, bf16),
        in_specs=[pl.BlockSpec(memory_space=pltpu.VMEM)] * 2,
        out_specs=pl.BlockSpec(memory_space=pltpu.VMEM),
        scratch_shapes=[
            pltpu.VMEM(shape, bf16),
            pltpu.VMEM(shape, bf16),
            dma((chunks,)),
            dma((chunks,)),
        ],
        compiler_params=pltpu.CompilerParams(collective_id=1, has_side_effects=True),
        cost_estimate=pl.CostEstimate(
            flops=2 * block.size, bytes_accessed=60 * block.size, transcendentals=0
        ),
        name="carry",
    )(spread, block.reshape(shape))
    return carried.reshape(heads, p, n)


def partner(place, bits):
    bit = 1
    while bit <= bits:
        if bits & bit:
            place = place + bit - 2 * bit * ((place // bit) % 2)
        bit *= 2
    return place


def project_kernel(
    sizes, hid, weight, out, w_buf, got, part, landed, summed,
    w_sem, ag_send, ag_recv, z_send, z_recv, o_send, o_recv,
):
    sections, shards, heads = sizes
    halves, count, _ = hid.shape
    rows, width = part.shape[3], part.shape[4]
    tile = min(512, width)
    here_s, here_h = lax.axis_index("seq"), lax.axis_index("head")
    other = lax.rem(lax.axis_index("section") + 1, sections)
    load = pltpu.make_async_copy(weight, w_buf, w_sem)
    load.start()
    barrier = pltpu.get_barrier_semaphore()
    for d in range(shards):
        if d:
            pl.semaphore_signal(barrier, inc=1, device_id={"seq": partner(here_s, d)})
        pl.semaphore_signal(
            barrier, inc=1, device_id={"section": other, "seq": partner(here_s, d)}
        )
    for e in range(1, heads):
        pl.semaphore_signal(barrier, inc=1, device_id={"head": partner(here_h, e)})
    pl.semaphore_wait(barrier, 2 * shards - 1 + heads - 1)

    def gather(q, d):
        return pltpu.make_async_remote_copy(
            hid.at[q], got.at[q, d - 1], ag_send.at[q, d], ag_recv.at[q, d],
            device_id={"seq": partner(here_s, d)},
        )

    bits = [1 << k for k in range(heads.bit_length() - 1)]

    def exchange(q, d, bit):
        first = heads - heads // bit
        return [
            pltpu.make_async_remote_copy(
                part.at[q, d, partner(here_h, e + bit)], landed.at[q, d, first + n],
                z_send.at[q, d, first + n], z_recv.at[q, d, first + n],
                device_id={"head": partner(here_h, bit)},
            )
            for n, e in enumerate(range(0, heads, 2 * bit))
        ]

    def deliver(q, d):
        return pltpu.make_async_remote_copy(
            summed.at[q, d], out.at[q, here_s], o_send.at[q, d], o_recv.at[q, d],
            device_id={"section": other, "seq": partner(here_s, d)},
        )

    for q in range(halves):
        for d in range(1, shards):
            gather(q, d).start()
    load.wait()

    def multiply(q, d):
        rows_in = hid.at[q] if d == 0 else got.at[q, d - 1]

        def one(i, _):
            cols = pl.ds(pl.multiple_of(i * tile, tile), tile)
            terms = jnp.dot(rows_in[...], w_buf[:, cols], preferred_element_type=jnp.float32)
            part[q, d, :, :, cols] = terms.astype(jnp.bfloat16).reshape(heads, rows, tile)
            return 0

        lax.fori_loop(0, width // tile, one, 0)

    def advance(q, d, k):
        bit = bits[k]
        first = heads - heads // bit
        for n, copy in enumerate(exchange(q, d, bit)):
            copy.wait_recv()
            mine = partner(here_h, 2 * bit * n)
            total = part[q, d, mine].astype(jnp.float32)
            total = (total + landed[q, d, first + n].astype(jnp.float32)).astype(jnp.bfloat16)
            if k + 1 < len(bits):
                part[q, d, mine] = total
            else:
                summed[q, d] = total
        if k + 1 < len(bits):
            for copy in exchange(q, d, bits[k + 1]):
                copy.start()
        else:
            deliver(q, d).start()

    units = [(q, 0) for q in range(halves)]
    units += [(q, d) for q in range(halves) for d in range(1, shards)]
    for n in range(len(units) + len(bits)):
        if n < len(units):
            q, d = units[n]
            if d:
                gather(q, d).wait_recv()
            multiply(q, d)
            for copy in exchange(q, d, bits[0]):
                copy.start()
        for k in range(len(bits)):
            if 0 <= n - 1 - k < len(units):
                advance(*units[n - 1 - k], k)
    for q, d in units:
        if d:
            gather(q, d).wait_send()
        for bit in bits:
            for copy in exchange(q, d, bit):
                copy.wait_send()
        deliver(q, d).wait_send()
        pltpu.make_async_remote_copy(
            summed.at[q, d], out.at[q, partner(here_s, d)], o_send.at[q, d], o_recv.at[q, d],
            device_id={"section": other, "seq": partner(here_s, d)},
        ).wait_recv()


def project(hid, weight, sizes):
    sections, shards, heads = sizes
    halves, count, depth = hid.shape
    width = weight.shape[1]
    rows = count // heads
    bf16 = jnp.bfloat16
    dma = pltpu.SemaphoreType.DMA
    flops = 2 * halves * count * shards * depth * width
    return pl.pallas_call(
        functools.partial(project_kernel, sizes),
        out_shape=jax.ShapeDtypeStruct((halves, shards, rows, width), bf16),
        in_specs=[pl.BlockSpec(memory_space=pltpu.VMEM), pl.BlockSpec(memory_space=pl.ANY)],
        out_specs=pl.BlockSpec(memory_space=pl.ANY),
        scratch_shapes=[
            pltpu.VMEM(weight.shape, bf16),
            pltpu.VMEM((halves, shards - 1, count, depth), bf16),
            pltpu.VMEM((halves, shards, heads, rows, width), bf16),
            pltpu.VMEM((halves, shards, heads - 1, rows, width), bf16),
            pltpu.VMEM((halves, shards, rows, width), bf16),
            dma,
            dma((halves, shards)),
            dma((halves, shards)),
            dma((halves, shards, heads)),
            dma((halves, shards, heads)),
            dma((halves, shards)),
            dma((halves, shards)),
        ],
        compiler_params=pltpu.CompilerParams(
            collective_id=0, has_side_effects=True, vmem_limit_bytes=48 * 2**20
        ),
        cost_estimate=pl.CostEstimate(
            flops=flops, bytes_accessed=2 * weight.size, transcendentals=0
        ),
        name="project",
    )(hid, weight)


def conv_silu(padded, kernel, length):
    kernel_taps = kernel.shape[0]
    summed = jnp.zeros((length, padded.shape[1]), jnp.float32)
    for offset in range(kernel_taps):
        summed = summed + kernel[offset] * padded[offset : offset + length].astype(jnp.float32)
    return jax.nn.silu(summed).astype(jnp.bfloat16)


def per_device(
    x_in,
    b_in,
    c_in,
    z_in,
    dt_raw,
    conv_x,
    conv_b,
    conv_c,
    a_rate,
    dt_bias,
    skip_d,
    norm_gain,
    out_weight,
):
    x_local = x_in[0]
    b_local = b_in[0]
    c_local = c_in[0]
    length = x_local.shape[0]
    kernel_taps = conv_x.shape[1]
    x_cols = x_local.shape[1]
    b_cols = b_local.shape[1]
    edge_rows = jnp.concatenate(
        [
            x_local[length - kernel_taps + 1 :],
            b_local[length - kernel_taps + 1 :],
            c_local[length - kernel_taps + 1 :],
        ],
        axis=1,
    )
    before = passed_along(edge_rows, "seq", 1)
    x_conv = conv_silu(jnp.concatenate([before[:, :x_cols], x_local], axis=0), conv_x[0], length)
    b_conv = conv_silu(
        jnp.concatenate([before[:, x_cols : x_cols + b_cols], b_local], axis=0), conv_b[0], length
    )
    c_conv = conv_silu(
        jnp.concatenate([before[:, x_cols + b_cols :], c_local], axis=0), conv_c[0], length
    )
    head_count = dt_raw.shape[1]
    group_count = b_cols // N
    per_group = head_count // group_count
    head_dim = x_cols // head_count
    step_size = jax.nn.softplus(dt_raw[0] + dt_bias[0][:, None])
    log_decay = jnp.cumsum(-a_rate[0][:, None] * step_size, axis=1)
    x_groups = x_conv.reshape(length, group_count, per_group, head_dim)
    b_groups = b_conv.reshape(length, group_count, N)
    c_groups = c_conv.reshape(length, group_count, N)
    log_groups = log_decay.reshape(group_count, per_group, length)
    step_groups = step_size.reshape(group_count, per_group, length)
    scores = jnp.einsum("tgn,ugn->gtu", c_groups, b_groups, preferred_element_type=jnp.float32)
    causal = jnp.arange(length)[:, None] >= jnp.arange(length)[None, :]
    spread_log = log_groups[:, :, :, None] - log_groups[:, :, None, :]
    damping = jnp.where(causal, jnp.exp(jnp.minimum(spread_log, 0.0)), 0.0)
    weights = (damping * step_groups[:, :, None, :] * scores[:, None]).astype(jnp.bfloat16)
    inside = jnp.einsum("gjtu,ugjp->tgjp", weights, x_groups, preferred_element_type=jnp.float32)
    to_end = jnp.exp(log_groups[:, :, -1:] - log_groups) * step_groups
    x_weighted = (
        x_groups.astype(jnp.float32) * jnp.transpose(to_end, (2, 0, 1))[..., None]
    ).astype(jnp.bfloat16)
    block_sum = jnp.einsum(
        "ugjp,ugn->gjpn", x_weighted, b_groups, preferred_element_type=jnp.float32
    )
    block_decay = jnp.exp(log_groups[:, :, -1])
    carried_b = entering(
        block_decay.reshape(-1),
        block_sum.reshape(head_count, head_dim, N),
        lax.axis_size("seq"),
    ).reshape(block_sum.shape)
    outside = jnp.einsum("tgn,gjpn->tgjp", c_groups, carried_b, preferred_element_type=jnp.float32)
    outside = outside * jnp.transpose(jnp.exp(log_groups), (2, 0, 1))[..., None]
    skip_term = skip_d[0].reshape(group_count, per_group)
    out_ssm = inside + outside + skip_term[None, :, :, None] * x_groups.astype(jnp.float32)
    gate_act = jax.nn.silu(z_in[0].astype(jnp.float32)).reshape(
        length, group_count, per_group * head_dim
    )
    gated = out_ssm.reshape(length, group_count, per_group * head_dim) * gate_act
    inverse_rms = lax.rsqrt(jnp.mean(gated * gated, axis=2, keepdims=True) + epsilon)
    hidden = ((gated * inverse_rms).reshape(length, x_cols) * norm_gain[0]).astype(jnp.bfloat16)
    sizes = tuple(lax.axis_size(name) for name in ("section", "seq", "head"))
    halves, heads = 2, sizes[2]
    rows = length // (heads * halves)
    hid = jnp.transpose(hidden.reshape(heads, halves, rows, x_cols), (1, 0, 2, 3))
    mixed = project(hid.reshape(halves, heads * rows, x_cols), out_weight[0], sizes)
    return jnp.transpose(mixed, (0, 2, 1, 3)).reshape(1, halves * rows, -1)


def solution(mesh):
    return jax.shard_map(
        per_device,
        mesh=mesh,
        in_specs=(
            P("section", "seq", "head"),
            P("section", "seq", "head"),
            P("section", "seq", "head"),
            P("section", "seq", "head"),
            P("section", "head", "seq"),
            P("section", None, "head"),
            P("section", None, "head"),
            P("section", None, "head"),
            P("section", "head"),
            P("section", "head"),
            P("section", "head"),
            P("section", "head"),
            P("section", "head", "seq"),
        ),
        out_specs=P("section", ("seq", "head"), None),
        check_vma=False,
    )
```

profile of v0, /device:TPU:1, one launch (start us, length us, event | category | flops | bytes accessed | tf_op | source)
XLA Modules:
  0.0 174.0 jit_solution(13222952578003400487)
XLA Ops:
  0.0 0.9 slice_bitcast_fusion
  0.9 0.7 slice_bitcast_fusion.1
  1.6 3.9 %collective-permute-start = (bf16[3,3072]{1,0:T(4,128)(2,1)S(1)}, bf16[3,3072]{1,0:T(4,128)(2,1)S(1)}, u32[]{:S(2)}, u32[]{:S(2)}) collective-permute-start(bf16[3,3072]{1,0:T(4,128)(2,1)S(1)} %pad_maximum_fusion.3), channel_id=1, source_target_pairs={{0,4},{4,8},{8,12},{1,5},{5,9},{9,13},{2,6},{6,10},{10,14},{3,7},{... | collective-permute-start | bytes 55304 | tf_op jit(solution)/shard_map/ppermute | solution.py:20
  5.5 0.9 fusion.34
  6.4 1.5 fusion.31
  7.9 0.8 squeeze.23
  8.7 0.7 negate_bitcast_fusion
  9.4 0.7 fusion.29
  10.1 0.6 reduce-window.6
  10.7 0.2 slice_reduce_fusion
  10.9 0.1 broadcast_add_fusion
  11.1 0.2 slice_reduce_fusion.1
  11.3 0.5 broadcast.75
  11.8 1.3 reduce.13
  13.1 0.1 add.106
  13.2 1.4 fusion.33
  14.6 1.5 multiply_bitcast_fusion
  16.1 2.6 %copy.56 = f32[1,256,2048]{1,2,0:T(8,128)} copy(bf16[1,256,2048]{2,1,0:T(8,128)(2,1)} %param.16) | data formatting | bytes 3145728 | tf_op jit(solution)/shard_map/convert_element_type | solution.py:322
  18.7 0.0 copy-done
  18.7 0.0 copy-start.2
  18.7 1.6 convert_element_type.97
  20.3 0.7 exp.58
  21.0 0.0 copy-done.15
  21.0 0.7 reduce.14
  21.6 0.6 mul.279
  22.3 0.0 collective-permute-done
  22.3 0.6 fusion.32
  22.9 0.0 copy-done.4
  22.9 0.3 multiply_convert_fusion.6
  23.2 0.8 reshape.170
  24.0 0.0 copy-done.2
  24.0 2.2 %multiply_convert_fusion.3 = bf16[256,2048]{1,0:T(8,128)(2,1)S(1)} fusion(bf16[256,2048]{1,0:T(8,128)(2,1)S(1)} %bitcast.75, bf16[3,2048]{1,0:T(4,128)(2,1)S(1)} %slice.145, f32[2048]{0:T(1024)} %bitcast.83, f32[2048]{0:T(1024)} %bitcast.84, f32[2048]{0:T(1024)S(1)} %bitcast.82, f32[2048]{0:T(1024)S(1)} %bitcast.81), kind=kLoop, calls=%fused_computation.16 | loop fusion | flops 13107200 | bytes 2142208 | tf_op jit(solution)/shard_map/convert_element_type | solution.py:247
  26.2 0.0 copy-start.5
  26.2 0.0 copy-start.8
  26.2 0.0 copy-start.10
  26.2 0.0 copy-start.11
  26.2 0.0 copy-start.12
  26.3 0.0 copy-start.13
  26.3 0.0 copy-start.3
  26.3 0.5 copy.48
  26.8 0.3 copy-done.5
  27.2 0.0 copy-done.8
  27.2 0.0 copy-done.10
  27.2 0.0 copy-done.11
  27.2 0.0 copy-done.12
  27.2 0.4 multiply_convert_fusion.7
  27.5 0.1 reshape.169
  27.6 0.0 copy-done.3
  27.6 1.8 %fusion.12 = f32[2,16,64,256]{3,2,1,0:T(8,128)} fusion(bf16[256,2,16,64]{0,3,2,1:T(8,128)(2,1)S(1)} %bitcast.70, f32[256,2,16]{0,2,1:T(8,128)S(1)} %get-tuple-element.7, bf16[256,2,256,1]{2,1,0,3:T(2,128)(2,1)S(1)} %bitcast.76), kind=kOutput, calls=%fused_computation.21 | convolution fusion | flops 270008320 | bytes 3440640 | tf_op jit(solution)/shard_map/ugjp,ugn->gjpn/dot_general | solution.py:309
  29.4 0.7 broadcast_in_dim.9.decay
  30.1 25.6 %carry.1 = bf16[8,4,64,256]{3,2,1,0:T(8,128)(2,1)} custom-call(f32[8,4,1,256]{3,2,1,0:T(1,128)} %broadcast_in_dim.9.decay, f32[8,4,64,256]{3,2,1,0:T(8,128)} %bitcast.67), custom_call_target="tpu_custom_call" | custom-call | flops 1048576 | bytes 31457280 | tf_op jit(solution)/shard_map/carry/pallas_call | solution.py:68
  55.7 1.8 %fusion.14 = f32[2,16,64,256]{3,2,1,0:T(8,128)S(1)} fusion(bf16[256,2,256,1]{2,1,0,3:T(2,128)(2,1)S(1)} %bitcast.77, bf16[2,16,64,256]{3,2,1,0:T(8,128)(2,1)} %bitcast.69), kind=kOutput, calls=%fused_computation.23 | convolution fusion | flops 268435456 | bytes 3407872 | tf_op jit(solution)/shard_map/tgn,gjpn->tgjp/dot_general | solution.py:318
  57.6 0.2 fusion.22
  57.9 3.2 %multiply_reduce_fusion = (f32[256,2]{0,1:T(2,128)S(1)}, f32[256,2,16,64]{0,3,2,1:T(8,128)S(1)}) fusion(f32[256,2,16,64]{0,3,2,1:T(8,128)S(1)} %bitcast.74, bf16[256,2,16,64]{0,3,2,1:T(8,128)(2,1)S(1)} %bitcast.71, f32[2,16]{1,0:T(2,128)S(1)} %copy-done.16, f32[256,2,16]{0,2,1:T(8,128)S(1)} %copy-done.7, f32[2,16,64,256]{3,2,1,0:T(8,128)S(1)} %fusion.14, ...), kind=kOutput, calls=%fused_computation.15 | convolution fusion | flops 287309312 | bytes 8030336 | tf_op jit(solution)/shard_map/gjtu,ugjp->tgjp/dot_general | solution.py:304
  61.0 4.6 %copy.55 = f32[256,2,16,64]{3,2,1,0:T(8,128)} copy(f32[256,2,16,64]{0,3,2,1:T(8,128)S(1)} %get-tuple-element.25) | data formatting | bytes 4194304 | tf_op jit(solution)/shard_map/add | solution.py:321
  65.7 3.6 %reshape.171 = f32[4,2,32,2048]{3,2,1,0:T(8,128)S(1)} reshape(f32[256,2,16,64]{3,2,1,0:T(8,128)} %copy.55) | data formatting | bytes 4194304 | tf_op jit(solution)/shard_map/reshape | solution.py:325
  69.3 0.1 copy.57
  69.4 1.9 %mul.287 = f32[256,2,1024]{2,1,0:T(2,128)} broadcast(f32[256,2]{1,0:T(8,128)S(1)} %copy.57), dimensions={0,1} | broadcast | bytes 2099200 | tf_op jit(solution)/shard_map/mul | solution.py:327
  71.3 4.1 %mul.288 = f32[4,2,32,2048]{3,2,1,0:T(8,128)} reshape(f32[256,2,1024]{2,1,0:T(2,128)} %mul.287) | data formatting | bytes 4194304 | tf_op jit(solution)/shard_map/mul | solution.py:327
  75.4 2.9 %fusion.17 = bf16[2,4,32,2048]{3,2,0,1:T(8,128)(2,1)S(1)} fusion(f32[2048]{0:T(1024)S(1)} %bitcast.93, f32[4,2,32,2048]{3,2,1,0:T(8,128)} %mul.288, f32[4,2,32,2048]{3,2,1,0:T(8,128)S(1)} %reshape.171, f32[4,2,32,2048]{3,2,1,0:T(8,128)} %bitcast.68), kind=kLoop, calls=%fused_computation.26 | loop fusion | flops 4194304 | bytes 7348224 | tf_op jit(solution)/shard_map/transpose | solution.py:331
  78.3 0.1 copy.58
  78.5 93.1 %project.1 = bf16[2,4,32,2048]{3,2,1,0:T(8,128)(2,1)S(1)} custom-call(bf16[2,128,2048]{2,1,0:T(8,128)(2,1)S(1)} %bitcast.65, bf16[2048,2048]{1,0:T(8,128)(2,1)} %bitcast.95), custom_call_target="tpu_custom_call" | custom-call | flops 8589934592 | bytes 8388608 | tf_op jit(solution)/shard_map/project/pallas_call | solution.py:213
  171.5 0.8 copy.59
  172.4 1.6 reshape.173
  (24 shorter events, 0.2 us)
Async XLA Ops:
  0.0 18.7 %copy-start = (bf16[1,256,2048]{2,1,0:T(8,128)(2,1)S(1)}, bf16[1,256,2048]{2,1,0:T(8,128)(2,1)}, u32[]{:S(2)}) copy-start(bf16[1,256,2048]{2,1,0:T(8,128)(2,1)} %param.16) | copy-start | bytes 3145732
  1.6 20.7 %collective-permute-start = (bf16[3,3072]{1,0:T(4,128)(2,1)S(1)}, bf16[3,3072]{1,0:T(4,128)(2,1)S(1)}, u32[]{:S(2)}, u32[]{:S(2)}) collective-permute-start(bf16[3,3072]{1,0:T(4,128)(2,1)S(1)} %pad_maximum_fusion.3), channel_id=1, source_target_pairs={{0,4},{4,8},{8,12},{1,5},{5,9},{9,13},{2,6},{6,10},{10,14},{3,7},{... | collective-permute-start | bytes 55304 | tf_op jit(solution)/shard_map/ppermute | solution.py:20
  18.7 2.2 %copy-start.15 = (f32[1,32]{1,0:T(1,128)S(1)}, f32[1,32]{1,0:T(1,128)}, u32[]{:S(2)}) copy-start(f32[1,32]{1,0:T(1,128)} %param.23) | copy-start | bytes 388
  18.7 4.2 %copy-start.4 = (bf16[1,256,512]{2,1,0:T(8,128)(2,1)S(1)}, bf16[1,256,512]{2,1,0:T(8,128)(2,1)}, u32[]{:S(2)}) copy-start(bf16[1,256,512]{2,1,0:T(8,128)(2,1)} %param.14) | copy-start | bytes 786436
  18.7 5.3 %copy-start.2 = (bf16[1,256,2048]{2,1,0:T(8,128)(2,1)S(1)}, bf16[1,256,2048]{2,1,0:T(8,128)(2,1)}, u32[]{:S(2)}) copy-start(bf16[1,256,2048]{2,1,0:T(8,128)(2,1)} %param.13) | copy-start | bytes 3145732
  26.2 1.0 copy-start.5
  26.2 0.9 copy-start.8
  26.2 0.9 copy-start.10
  26.2 0.9 copy-start.11
  26.2 0.9 copy-start.12
  26.3 0.9 copy-start.13
  26.3 1.4 copy-start.3
  27.5 1.9 %copy-start.9 = (f32[8,4]{1,0:T(8,128)S(1)}, f32[8,4]{1,0:T(8,128)}, u32[]{:S(2)}) copy-start(f32[8,4]{1,0:T(8,128)} %exp.58) | copy-start | bytes 388
  55.7 2.1 %copy-start.1 = (f32[1,256,2048]{1,2,0:T(8,128)S(1)}, f32[1,256,2048]{1,2,0:T(8,128)}, u32[]{:S(2)}) copy-start(f32[1,256,2048]{1,2,0:T(8,128)} %copy.56) | copy-start | bytes 6291460
  55.7 2.1 %copy-start.6 = (f32[2,16,256]{2,1,0:T(8,128)S(1)}, f32[2,16,256]{2,1,0:T(8,128)}, u32[]{:S(2)}) copy-start(f32[2,16,256]{2,1,0:T(8,128)} %get-tuple-element.8) | copy-start | bytes 98308
  55.7 2.1 %copy-start.7 = (f32[256,2,16]{0,2,1:T(8,128)S(1)}, f32[256,2,16]{0,2,1:T(8,128)}, u32[]{:S(2)}) copy-start(f32[256,2,16]{0,2,1:T(8,128)} %get-tuple-element.9) | copy-start | bytes 98308
  55.7 2.1 %copy-start.16 = (f32[2,16]{1,0:T(2,128)S(1)}, f32[2,16]{1,0:T(2,128)}, u32[]{:S(2)}) copy-start(f32[2,16]{1,0:T(2,128)} %mul.279) | copy-start | bytes 388
  71.3 4.1 %copy-start.14 = (f32[1,2048]{1,0:T(1,128)S(1)}, f32[1,2048]{1,0:T(1,128)}, u32[]{:S(2)}) copy-start(f32[1,2048]{1,0:T(1,128)} %param.24) | copy-start | bytes 24580
where the time goes:
time: 176 us; the launch traced here: 174 us
  Pallas kernels  119 us (68%)
  local copies, waits for them, and re-layouts  31.1 us (18%)
  other arithmetic  13 us (7%)
  matrix products  7 us (4%)
  starting transfers between devices  3.93 us (2%)
    pallas_call x1, Pallas kernels, project(): pl.pallas_call(functools.partial(project_kernel, sizes), out_shape=jax.Sh...  93.1 us
    pallas_call x1, Pallas kernels, entering(): pl.pallas_call(functools.partial(carry_kernel, shards), out_shape=jax.Sha...  25.6 us
    mul x2, local copies, waits for them, and re-layouts, per_device(): gated * inverse_rms  5.99 us
    add x1, local copies, waits for them, and re-layouts, per_device(): inside + outside  4.64 us
    ppermute x1, starting transfers between devices, passed_along(): return lax.ppermute(block, axis, route)  3.93 us
    slice x3, local copies, waits for them, and re-layouts, conv_silu(): kernel[offset] * padded[offset:offset + length].astype(jnp.float32)  3.85 us
    reshape x1, local copies, waits for them, and re-layouts, per_device(): out_ssm.reshape(length, group_count, per_group * head_dim) * gate_act  3.6 us
  transfers between devices with their start and end apart: 1, of which 0 were waited for; matrix products, arithmetic and copies ran while one was open for 10% of the time, Pallas kernels for 0%

commit v1 on v0

v1 whole, which is shorter than its diff:
```python
import functools

import jax
import jax.numpy as jnp
from jax import lax
from jax.experimental import pallas as pl
from jax.experimental.pallas import tpu as pltpu
from jax.sharding import PartitionSpec as P

N = 256


epsilon = 1e-05


def partner(place, bits):
    bit = 1
    while bit <= bits:
        if bits & bit:
            place = place + bit - 2 * bit * ((place // bit) % 2)
        bit *= 2
    return place


def project_kernel(
    sizes, hid, weight, out, w_buf, got, part, landed, summed,
    w_sem, ag_send, ag_recv, z_send, z_recv, o_send, o_recv,
):
    sections, shards, heads = sizes
    halves, count, _ = hid.shape
    rows, width = part.shape[3], part.shape[4]
    tile = min(512, width)
    here_s, here_h = lax.axis_index("seq"), lax.axis_index("head")
    other = lax.rem(lax.axis_index("section") + 1, sections)
    load = pltpu.make_async_copy(weight, w_buf, w_sem)
    load.start()
    barrier = pltpu.get_barrier_semaphore()
    for d in range(shards):
        if d:
            pl.semaphore_signal(barrier, inc=1, device_id={"seq": partner(here_s, d)})
        pl.semaphore_signal(
            barrier, inc=1, device_id={"section": other, "seq": partner(here_s, d)}
        )
    for e in range(1, heads):
        pl.semaphore_signal(barrier, inc=1, device_id={"head": partner(here_h, e)})
    pl.semaphore_wait(barrier, 2 * shards - 1 + heads - 1)

    def gather(q, d):
        return pltpu.make_async_remote_copy(
            hid.at[q], got.at[q, d - 1], ag_send.at[q, d], ag_recv.at[q, d],
            device_id={"seq": partner(here_s, d)},
        )

    bits = [1 << k for k in range(heads.bit_length() - 1)]

    def exchange(q, d, bit):
        first = heads - heads // bit
        return [
            pltpu.make_async_remote_copy(
                part.at[q, d, partner(here_h, e + bit)], landed.at[q, d, first + n],
                z_send.at[q, d, first + n], z_recv.at[q, d, first + n],
                device_id={"head": partner(here_h, bit)},
            )
            for n, e in enumerate(range(0, heads, 2 * bit))
        ]

    def deliver(q, d):
        return pltpu.make_async_remote_copy(
            summed.at[q, d], out.at[q, here_s], o_send.at[q, d], o_recv.at[q, d],
            device_id={"section": other, "seq": partner(here_s, d)},
        )

    for q in range(halves):
        for d in range(1, shards):
            gather(q, d).start()
    load.wait()

    def multiply(q, d):
        rows_in = hid.at[q] if d == 0 else got.at[q, d - 1]

        def one(i, _):
            cols = pl.ds(pl.multiple_of(i * tile, tile), tile)
            terms = jnp.dot(rows_in[...], w_buf[:, cols], preferred_element_type=jnp.float32)
            part[q, d, :, :, cols] = terms.astype(jnp.bfloat16).reshape(heads, rows, tile)
            return 0

        lax.fori_loop(0, width // tile, one, 0)

    def advance(q, d, k):
        bit = bits[k]
        first = heads - heads // bit
        for n, copy in enumerate(exchange(q, d, bit)):
            copy.wait_recv()
            mine = partner(here_h, 2 * bit * n)
            total = part[q, d, mine].astype(jnp.float32)
            total = (total + landed[q, d, first + n].astype(jnp.float32)).astype(jnp.bfloat16)
            if k + 1 < len(bits):
                part[q, d, mine] = total
            else:
                summed[q, d] = total
        if k + 1 < len(bits):
            for copy in exchange(q, d, bits[k + 1]):
                copy.start()
        else:
            deliver(q, d).start()

    units = [(q, 0) for q in range(halves)]
    units += [(q, d) for q in range(halves) for d in range(1, shards)]
    for n in range(len(units) + len(bits)):
        if n < len(units):
            q, d = units[n]
            if d:
                gather(q, d).wait_recv()
            multiply(q, d)
            for copy in exchange(q, d, bits[0]):
                copy.start()
        for k in range(len(bits)):
            if 0 <= n - 1 - k < len(units):
                advance(*units[n - 1 - k], k)
    for q, d in units:
        if d:
            gather(q, d).wait_send()
        for bit in bits:
            for copy in exchange(q, d, bit):
                copy.wait_send()
        deliver(q, d).wait_send()
        pltpu.make_async_remote_copy(
            summed.at[q, d], out.at[q, partner(here_s, d)], o_send.at[q, d], o_recv.at[q, d],
            device_id={"section": other, "seq": partner(here_s, d)},
        ).wait_recv()


def project(hid, weight, sizes):
    sections, shards, heads = sizes
    halves, count, depth = hid.shape
    width = weight.shape[1]
    rows = count // heads
    bf16 = jnp.bfloat16
    dma = pltpu.SemaphoreType.DMA
    flops = 2 * halves * count * shards * depth * width
    return pl.pallas_call(
        functools.partial(project_kernel, sizes),
        out_shape=jax.ShapeDtypeStruct((halves, shards, rows, width), bf16),
        in_specs=[pl.BlockSpec(memory_space=pltpu.VMEM), pl.BlockSpec(memory_space=pl.ANY)],
        out_specs=pl.BlockSpec(memory_space=pl.ANY),
        scratch_shapes=[
            pltpu.VMEM(weight.shape, bf16),
            pltpu.VMEM((halves, shards - 1, count, depth), bf16),
            pltpu.VMEM((halves, shards, heads, rows, width), bf16),
            pltpu.VMEM((halves, shards, heads - 1, rows, width), bf16),
            pltpu.VMEM((halves, shards, rows, width), bf16),
            dma,
            dma((halves, shards)),
            dma((halves, shards)),
            dma((halves, shards, heads)),
            dma((halves, shards, heads)),
            dma((halves, shards)),
            dma((halves, shards)),
        ],
        compiler_params=pltpu.CompilerParams(
            collective_id=0, has_side_effects=True, vmem_limit_bytes=48 * 2**20
        ),
        cost_estimate=pl.CostEstimate(
            flops=flops, bytes_accessed=2 * weight.size, transcendentals=0
        ),
        name="project",
    )(hid, weight)


def mix_kernel(
    shards, dims, x_hbm, b_hbm, c_hbm, z_hbm, dt_hbm, kx_hbm, kb_hbm, kc_hbm, a_hbm, bias_hbm,
    skip_hbm, gain_hbm, hid, x, b, c, z, dt, kx, kb, kc, a, bias, skip, gain, loaded,
    ex, eb, ec, pad, xc, bt, cc, sc, vec, dtp, ldrow, steprow, ldcol, cat, tocat,
    eld, sums, acc, ssq, inbox, outbox, e_send, e_recv, send, recv,
):
    head_dim, chunk, heads_z, halves = dims
    f32, bf16 = jnp.float32, jnp.bfloat16
    me = lax.axis_index("seq")
    length, width = x.shape
    head_count = dt.shape[0]
    groups = sc.shape[0]
    state = bt.shape[1]
    taps = kx.shape[0]
    edge = ex.shape[0]
    chunks = width // chunk
    per_chunk = chunk // head_dim
    group_chunks = chunks // groups
    lanes = 128
    after, before = lax.rem(me + 1, shards), lax.rem(me + shards - 1, shards)
    first, last = me == 0, me == shards - 1
    froms = (b_hbm, c_hbm, x_hbm, dt_hbm, kx_hbm, kb_hbm, kc_hbm, a_hbm, bias_hbm, skip_hbm)
    tos = (b, c, x, dt, kx, kb, kc, a, bias, skip)
    froms, tos = froms + (z_hbm, gain_hbm), tos + (z, gain)
    loads = [
        pltpu.make_async_copy(src, dst, loaded.at[n])
        for n, (src, dst) in enumerate(zip(froms, tos))
    ]
    for load in loads:
        load.start()
    barrier = pltpu.get_barrier_semaphore()
    for neighbour in (before, after):
        pl.semaphore_signal(barrier, inc=1, device_id={"seq": neighbour})
    pl.semaphore_wait(barrier, 2)

    edges = [
        pltpu.make_async_remote_copy(
            src.at[pl.ds(length - edge, edge)], dst, e_send.at[n], e_recv.at[n],
            device_id={"seq": after},
        )
        for n, (src, dst) in enumerate(((x_hbm, ex), (b_hbm, eb), (c_hbm, ec)))
    ]

    def hand_on(k):
        return pltpu.make_async_remote_copy(
            outbox.at[k], inbox.at[k], send.at[k], recv.at[k], device_id={"seq": after}
        )

    @pl.when(jnp.logical_not(last))
    def _():
        for copy in edges:
            copy.start()

    @pl.when(first)
    def _():
        for dst in (ex, eb, ec):
            dst[...] = jnp.zeros(dst.shape, dst.dtype)

    for load in loads:
        load.wait()

    vec[...] = jnp.zeros(vec.shape, f32)
    dtp[...] = jnp.zeros(dtp.shape, f32)
    dtp[:head_count, :] = dt[...]
    for n, ref in enumerate((a, bias, skip)):
        vec[8 * n : 8 * n + 1, :head_count] = ref[...]
    step = jax.nn.softplus(dtp[...].T + vec[8:9, :])
    rows = lax.broadcasted_iota(jnp.int32, (length, length), 0)
    columns = lax.broadcasted_iota(jnp.int32, (length, length), 1)
    causal = rows >= columns
    decay = jnp.dot(
        jnp.where(causal, 1.0, 0.0), -vec[0:1, :] * step,
        precision=lax.Precision.HIGHEST, preferred_element_type=f32,
    )
    ldrow[...] = decay.T
    steprow[...] = step.T
    for k in range(chunks):
        ldcol[k] = decay[:, k * per_chunk : (k + 1) * per_chunk]

    def split(dst, value, first_row):
        size = value.shape[0]
        for n in range(3):
            part = value.astype(bf16)
            dst[n, first_row : first_row + size, :] = part
            value = value - part.astype(f32)

    split(cat, jnp.exp(decay), 0)
    split(cat, jnp.broadcast_to(vec[16:17, :], (16, lanes)), length)
    split(tocat, jnp.exp(decay[length - 1 : length, :] - decay) * step, 0)

    def conv(src, border, kernel, cols):
        pad[0:edge, :] = border[:, cols].astype(f32)
        pad[edge:, :] = src[:, cols].astype(f32)
        total = jnp.zeros((length, pad.shape[1]), f32)
        for k in range(taps):
            start = edge - taps + 1 + k
            total = total + kernel[k : k + 1, cols] * pad[start : start + length, :]
        return total * jax.nn.sigmoid(total)

    @pl.when(me > 0)
    def _():
        for copy in edges:
            copy.wait_recv()

    for g in range(groups):
        cols = slice(g * state, (g + 1) * state)
        b_conv = conv(b, eb, kb, cols).astype(bf16)
        bt[g] = b_conv.astype(f32).T.astype(bf16)
        cc[:, cols] = conv(c, ec, kc, cols).astype(bf16)
        scores = jnp.dot(cc[:, cols], bt[g], preferred_element_type=f32)
        sc[g] = jnp.where(causal, scores, 0.0)

    def spread(src, k):
        head = lax.broadcasted_iota(jnp.int32, (lanes, chunk), 0) - k * per_chunk
        lane = lax.broadcasted_iota(jnp.int32, (lanes, chunk), 1)
        start = head * head_dim
        pick = jnp.where((lane >= start) & (lane < start + head_dim), 1.0, 0.0).astype(bf16)
        total = jnp.dot(src[0], pick, preferred_element_type=f32)
        for n in range(1, 3):
            total = total + jnp.dot(src[n], pick, preferred_element_type=f32)
        return total

    def gather_state(k, _):
        cols = pl.ds(pl.multiple_of(k * chunk, chunk), chunk)
        x_conv = conv(x, ex, kx, cols).astype(bf16)
        xc[:, cols] = x_conv
        eld[:, cols] = spread(cat, k)
        weighted = (x_conv.astype(f32) * spread(tocat, k)).astype(bf16)
        total = jnp.dot(bt[k // group_chunks], weighted, preferred_element_type=f32)
        sums[:, cols] = total

        @pl.when(first)
        def _():
            outbox[k] = total.astype(bf16)
            hand_on(k).start()

        return 0

    lax.fori_loop(0, chunks, gather_state, 0)
    per_tile = lanes // head_dim

    def finish(k, _):
        cols = pl.ds(pl.multiple_of(k * chunk, chunk), chunk)
        g = k // group_chunks
        scores = sc[g]
        columns_of = ldcol[k]
        for j in range(chunk // lanes):
            tile = pl.ds(pl.multiple_of(k * chunk + j * lanes, lanes), lanes)
            x_tile = xc[:, tile]
            lane = lax.broadcasted_iota(jnp.int32, (length, lanes), 1)
            inside = None
            for i in range(per_tile):
                n = j * per_tile + i
                h = k * per_chunk + n
                gap = columns_of[:, n : n + 1] - ldrow[pl.ds(h, 1), :]
                damping = jnp.exp(jnp.minimum(gap, 0.0))
                weights = (damping * steprow[pl.ds(h, 1), :] * scores).astype(bf16)
                term = jnp.dot(weights, x_tile, preferred_element_type=f32)
                inside = term if i == 0 else jnp.where(lane >= i * head_dim, term, inside)
            acc[:, tile] = inside

        @pl.when(me > 0)
        def _():
            hand_on(k).wait_recv()

            @pl.when(jnp.logical_not(last))
            def _():
                old = eld[length - 1 : length, cols] * inbox[k].astype(f32)
                outbox[k] = (old + sums[:, cols]).astype(bf16)
                hand_on(k).start()

            c_group = cc[:, pl.ds(pl.multiple_of(g * state, state), state)]
            outside = jnp.dot(c_group, inbox[k], preferred_element_type=f32)
            acc[:, cols] = acc[:, cols] + outside * eld[:length, cols]

        z_here = z[:, cols].astype(f32)
        total = acc[:, cols] + eld[length : length + 1, cols] * xc[:, cols].astype(f32)
        gated = total * (z_here * jax.nn.sigmoid(z_here))
        acc[:, cols] = gated
        square = gated * gated
        part = square[:, :lanes]
        for j in range(1, chunk // lanes):
            part = part + square[:, j * lanes : (j + 1) * lanes]
        ssq[...] = jnp.where(lax.rem(k, group_chunks) == 0, part, ssq[...] + part)

        @pl.when(lax.rem(k, group_chunks) == group_chunks - 1)
        def _():
            mean = jnp.sum(ssq[...], axis=1, keepdims=True) / (group_chunks * chunk)
            scale = lax.rsqrt(mean + epsilon)
            count = length // (heads_z * halves)
            for j in range(group_chunks):
                first_col = (k - group_chunks + 1 + j) * chunk
                here = pl.ds(pl.multiple_of(first_col, chunk), chunk)
                value = (acc[:, here] * scale * gain[:, here]).astype(bf16)
                for e in range(heads_z):
                    for q in range(halves):
                        row = (e * halves + q) * count
                        hid[q, e * count : (e + 1) * count, here] = value[row : row + count]

        return 0

    lax.fori_loop(0, chunks, finish, 0)

    @pl.when(jnp.logical_not(last))
    def _():
        for copy in edges:
            copy.wait_send()

        def drain(k, _):
            hand_on(k).wait_send()
            return 0

        lax.fori_loop(0, chunks, drain, 0)


def mix(args, sizes, halves):
    x, b, c, z, dt, kx, kb, kc, a, bias, skip, gain = args
    sections, shards, heads_z = sizes
    length, width = x.shape
    head_count = dt.shape[0]
    head_dim = width // head_count
    groups = b.shape[1] // N
    chunk, lanes, edge = 256, 128, 8
    chunks = width // chunk
    f32, bf16 = jnp.float32, jnp.bfloat16
    dma = pltpu.SemaphoreType.DMA
    vmem = pltpu.VMEM
    count = length // halves
    return pl.pallas_call(
        functools.partial(mix_kernel, shards, (head_dim, chunk, heads_z, halves)),
        out_shape=jax.ShapeDtypeStruct((halves, count, width), bf16),
        in_specs=[pl.BlockSpec(memory_space=pl.ANY)] * 12,
        out_specs=pl.BlockSpec(memory_space=vmem),
        scratch_shapes=[vmem(array.shape, array.dtype) for array in args]
        + [
            dma((12,)),
            vmem((edge, width), bf16),
            vmem((edge, b.shape[1]), bf16),
            vmem((edge, b.shape[1]), bf16),
            vmem((edge + length, chunk), f32),
            vmem((length, width), bf16),
            vmem((groups, N, length), bf16),
            vmem((length, groups * N), bf16),
            vmem((groups, length, length), f32),
            vmem((24, lanes), f32),
            vmem((lanes, length), f32),
            vmem((lanes, length), f32),
            vmem((lanes, length), f32),
            vmem((chunks, length, chunk // head_dim), f32),
            vmem((3, length + 16, lanes), bf16),
            vmem((3, length, lanes), bf16),
            vmem((length + 16, width), f32),
            vmem((N, width), f32),
            vmem((length, width), f32),
            vmem((length, lanes), f32),
            vmem((chunks, N, chunk), bf16),
            vmem((chunks, N, chunk), bf16),
            dma((3,)),
            dma((3,)),
            dma((chunks,)),
            dma((chunks,)),
        ],
        compiler_params=pltpu.CompilerParams(
            collective_id=1, has_side_effects=True, vmem_limit_bytes=63 * 2**20
        ),
        cost_estimate=pl.CostEstimate(
            flops=2 * length * length * width * 4, bytes_accessed=8 * x.size, transcendentals=0
        ),
        name="mix",
    )(*args)


def per_device(
    x_in,
    b_in,
    c_in,
    z_in,
    dt_raw,
    conv_x,
    conv_b,
    conv_c,
    a_rate,
    dt_bias,
    skip_d,
    norm_gain,
    out_weight,
):
    sizes = tuple(lax.axis_size(name) for name in ("section", "seq", "head"))
    halves = 2
    whole = (x_in, b_in, c_in, z_in, dt_raw, conv_x, conv_b, conv_c)
    args = [array[0] for array in whole] + [a_rate, dt_bias, skip_d, norm_gain]
    hid = mix(args, sizes, halves)
    rows = x_in.shape[1] // (sizes[2] * halves)
    mixed = project(hid, out_weight[0], sizes)
    return jnp.transpose(mixed, (0, 2, 1, 3)).reshape(1, halves * rows, -1)


def solution(mesh):
    return jax.shard_map(
        per_device,
        mesh=mesh,
        in_specs=(
            P("section", "seq", "head"),
            P("section", "seq", "head"),
            P("section", "seq", "head"),
            P("section", "seq", "head"),
            P("section", "head", "seq"),
            P("section", None, "head"),
            P("section", None, "head"),
            P("section", None, "head"),
            P("section", "head"),
            P("section", "head"),
            P("section", "head"),
            P("section", "head"),
            P("section", "head", "seq"),
        ),
        out_specs=P("section", ("seq", "head"), None),
        check_vma=False,
    )
```

time: 176 us -> 130 us (0.74)
  local copies, waits for them, and re-layouts: 31.1 us -> 3.63 us
  other arithmetic: 13 us -> 0 us
  matrix products: 7 us -> 0 us
  Pallas kernels: 119 us -> 125 us
  starting transfers between devices: 3.93 us -> 0 us
    dot_general x4 -> x0, matrix products: 7 us -> none  [the longest x1 3.15 us: per_device(): jnp.einsum('gjtu,ugjp->tgjp', weights, x_groups, preferred_element_type=j...]
    mul x3 -> x0, local copies, waits for them, and re-layouts: 6.64 us -> none  [the longest x2 5.99 us: per_device(): gated * inverse_rms]
    slice x9 -> x0, local copies, waits for them, and re-layouts: 6.36 us -> none  [the longest x3 3.85 us: conv_silu(): kernel[offset] * padded[offset:offset + length].astype(jnp.float32)]
    add x2 -> x0, local copies, waits for them, and re-layouts: 4.73 us -> none  [the longest x1 4.64 us: per_device(): inside + outside]
    reshape x3 -> x0, local copies, waits for them, and re-layouts: 4.43 us -> none  [the longest x1 3.6 us: per_device(): out_ssm.reshape(length, group_count, per_group * head_dim) * gate_act]
    convert_element_type x4 -> x0, other arithmetic: 4.43 us -> none  [the longest x3 2.88 us: conv_silu(): return jax.nn.silu(summed).astype(jnp.bfloat16)]
    transpose x2 -> x0, other arithmetic: 4.39 us -> none  [the longest x1 2.92 us: per_device(): jnp.transpose(hidden.reshape(heads, halves, rows, x_cols), (1, 0, 2, 3))]
    ppermute x1 -> x0, starting transfers between devices: 3.93 us -> none  [passed_along(): return lax.ppermute(block, axis, route)]
  transfers between devices with their start and end apart: 1 -> 0, of which waited for: 0 -> 0; matrix products, arithmetic and copies ran while one was open for 10% -> 0% of each run, Pallas kernels for 0% -> 0%
where the time goes in v1:
time: 130 us; the launch traced here: 128 us
  Pallas kernels  125 us (96%)
  local copies, waits for them, and re-layouts  3.63 us (3%)
    pallas_call x1, Pallas kernels, project(): pl.pallas_call(functools.partial(project_kernel, sizes), out_shape=jax.Sh...  95.8 us
    pallas_call x1, Pallas kernels, mix(): pl.pallas_call(functools.partial(mix_kernel, shards, (head_dim, chunk, he...  28.8 us

profile of v1, /device:TPU:1, one launch (start us, length us, event | category | flops | bytes accessed | tf_op | source)
XLA Modules:
  0.0 128.2 jit_solution(2080998347981846863)
XLA Ops:
  0.0 28.8 %mix.1.hid = bf16[2,128,2048]{2,1,0:T(8,128)(2,1)} custom-call(bf16[256,2048]{1,0:T(8,128)(2,1)} %bitcast.12, bf16[256,512]{1,0:T(8,128)(2,1)} %bitcast.14, bf16[256,512]{1,0:T(8,128)(2,1)} %bitcast.15, bf16[256,2048]{1,0:T(8,128)(2,1)} %bitcast.13, f32[32,256]{1,0:T(8,128)} %bitcast.16, f32[4,2048]{1,0:T(4,128)} %bitcast.17, f32[4,512]{1,0:T(4,128)} %bitcast.18, ...), custom_call_target="tpu_custom_call" | custom-call | flops 1073741824 | bytes 4194304 | tf_op jit(solution)/shard_map/mix/pallas_call | solution.py:398
  28.8 0.0 copy-start
  28.8 1.2 copy-done
  30.0 95.8 %project.1 = bf16[2,4,32,2048]{3,2,1,0:T(8,128)(2,1)S(1)} custom-call(bf16[2,128,2048]{2,1,0:T(8,128)(2,1)S(1)} %copy-done, bf16[2048,2048]{1,0:T(8,128)(2,1)} %bitcast.11), custom_call_target="tpu_custom_call" | custom-call | flops 8589934592 | bytes 8388608 | tf_op jit(solution)/shard_map/project/pallas_call | solution.py:141
  125.8 0.8 copy.14
  126.6 1.6 %reshape.3 = bf16[1,64,8192]{2,1,0:T(8,128)(2,1)} reshape(bf16[2,32,4,2048]{3,2,1,0:T(4,128)(2,1)S(1)} %copy.14) | data formatting | bytes 2097152 | tf_op jit(solution)/shard_map/reshape | solution.py:464
Async XLA Ops:
  28.8 1.2 copy-start

commit v2 on v1

v2 whole, which is shorter than its diff:
```python
import functools

import jax
import jax.numpy as jnp
from jax import lax
from jax.experimental import pallas as pl
from jax.experimental.pallas import tpu as pltpu
from jax.sharding import PartitionSpec as P

N = 256


epsilon = 1e-05


def partner(place, bits, size):
    bit = 1
    while bit < size:
        flip = (bits // bit) % 2
        place = place + flip * (bit - 2 * bit * ((place // bit) % 2))
        bit *= 2
    return place


def layer_kernel(
    sizes, dims, x_hbm, b_hbm, c_hbm, z_hbm, dt_hbm, kx_hbm, kb_hbm, kc_hbm, a_hbm, bias_hbm,
    skip_hbm, gain_hbm, weight, out, x, b, c, z, dt, kx, kb, kc, a, bias, skip, gain, loaded,
    ex, eb, ec, pad, xc, bt, cc, sc, vec, dtp, ldrow, steprow, ldcol, cat, tocat,
    eld, sums, acc, ssq, inbox, outbox, e_send, e_recv, send, recv,
    w_buf, got, part, up, down,
    w_sem, ag_send, ag_recv, u_send, u_recv, d_send, d_recv, o_send, o_recv,
):
    sections, shards, heads = sizes
    head_dim, chunk, halves, lag = dims
    count = got.shape[1]
    units = shards * halves
    rows, width = part.shape[2], part.shape[3]
    tile = min(512, width)
    tiles = width // tile
    f32, bf16 = jnp.float32, jnp.bfloat16
    here_s, h_z = lax.axis_index("seq"), lax.axis_index("head")
    end = heads - 1
    other = lax.rem(lax.axis_index("section") + 1, sections)
    me = here_s
    length, inner = x.shape
    head_count = dt.shape[0]
    groups = sc.shape[0]
    state = bt.shape[1]
    taps = kx.shape[0]
    edge = ex.shape[0]
    chunks = inner // chunk
    per_chunk = chunk // head_dim
    group_chunks = chunks // groups
    lanes = 128
    after, before = lax.rem(me + 1, shards), lax.rem(me + shards - 1, shards)
    first, last = me == 0, me == shards - 1
    froms = (dt_hbm, a_hbm, bias_hbm, skip_hbm, kb_hbm, kx_hbm, b_hbm, x_hbm)
    tos = (dt, a, bias, skip, kb, kx, b, x)
    small, early = 4, len(tos)
    froms, tos = froms + (kc_hbm, c_hbm, z_hbm, gain_hbm), tos + (kc, c, z, gain)
    loads = [
        pltpu.make_async_copy(src, dst, loaded.at[n])
        for n, (src, dst) in enumerate(zip(froms, tos))
    ]
    for load in loads:
        load.start()
    w_loads = [
        pltpu.make_async_copy(
            weight.at[:, pl.ds(i * tile, tile)], w_buf.at[:, pl.ds(i * tile, tile)], w_sem.at[i]
        )
        for i in range(tiles)
    ]
    barrier = pltpu.get_barrier_semaphore()
    for d in range(shards):
        peer = partner(here_s, d, shards)
        if d:
            pl.semaphore_signal(barrier, inc=1, device_id={"seq": peer})
        pl.semaphore_signal(barrier, inc=1, device_id={"section": other, "seq": peer})

    @pl.when(h_z > 0)
    def _():
        pl.semaphore_signal(barrier, inc=1, device_id={"head": h_z - 1})

    @pl.when(h_z < end)
    def _():
        pl.semaphore_signal(barrier, inc=1, device_id={"head": h_z + 1})

    near = jnp.where(h_z > 0, 1, 0) + jnp.where(h_z < end, 1, 0)
    pl.semaphore_wait(barrier, 2 * shards - 1 + near)

    edges = [
        pltpu.make_async_remote_copy(
            src.at[pl.ds(length - edge, edge)], dst, e_send.at[n], e_recv.at[n],
            device_id={"seq": after},
        )
        for n, (src, dst) in enumerate(((x_hbm, ex), (b_hbm, eb), (c_hbm, ec)))
    ]

    pieces = outbox.shape[1]
    piece = outbox.shape[3]

    def hand_on(k, i):
        return pltpu.make_async_remote_copy(
            outbox.at[k, i], inbox.at[k, i], send.at[k, i], recv.at[k, i],
            device_id={"seq": after},
        )

    @pl.when(jnp.logical_not(last))
    def _():
        for copy in edges:
            copy.start()

    @pl.when(first)
    def _():
        for dst in (ex, eb, ec):
            dst[...] = jnp.zeros(dst.shape, dst.dtype)

    for load in loads[:small]:
        load.wait()

    vec[...] = jnp.zeros(vec.shape, f32)
    dtp[...] = jnp.zeros(dtp.shape, f32)
    dtp[:head_count, :] = dt[...]
    for n, ref in enumerate((a, bias, skip)):
        vec[8 * n : 8 * n + 1, :head_count] = ref[...]
    step = jax.nn.softplus(dtp[...].T + vec[8:9, :])
    causal = lax.broadcasted_iota(jnp.int32, (length, length), 0) >= lax.broadcasted_iota(
        jnp.int32, (length, length), 1
    )
    below = jnp.where(causal, 1.0, 0.0).astype(bf16)
    rest = -vec[0:1, :] * step
    decay = jnp.zeros((length, lanes), f32)
    for _ in range(3):
        high = rest.astype(bf16)
        decay = decay + jnp.dot(below, high, preferred_element_type=f32)
        rest = rest - high.astype(f32)
    ldrow[...] = decay.T
    steprow[...] = step.T
    for k in range(chunks):
        ldcol[k] = decay[:, k * per_chunk : (k + 1) * per_chunk]

    def split(dst, value, first_row):
        size = value.shape[0]
        high = value.astype(bf16)
        dst[first_row : first_row + size, :lanes] = high
        dst[first_row : first_row + size, lanes:] = (value - high.astype(f32)).astype(bf16)

    split(cat, jnp.exp(decay), 0)
    split(cat, jnp.broadcast_to(vec[16:17, :], (16, lanes)), length)
    split(tocat, jnp.exp(decay[length - 1 : length, :] - decay) * step, 0)

    for load in loads[small:early]:
        load.wait()
    for load in w_loads:
        load.start()

    def conv(src, border, kernel, cols):
        pad[0:edge, :] = border[:, cols].astype(f32)
        pad[edge:, :] = src[:, cols].astype(f32)
        total = jnp.zeros((length, pad.shape[1]), f32)
        for k in range(taps):
            start = edge - taps + 1 + k
            total = total + kernel[k : k + 1, cols] * pad[start : start + length, :]
        return total * jax.nn.sigmoid(total)

    @pl.when(me > 0)
    def _():
        for copy in edges:
            copy.wait_recv()

    def ready(g):
        cols = pl.ds(pl.multiple_of(g * state, state), state)
        bt[g] = conv(b, eb, kb, cols).astype(bf16).astype(f32).T.astype(bf16)

    def spread(src, k):
        head = lax.broadcasted_iota(jnp.int32, (lanes, chunk), 0) - k * per_chunk
        lane = lax.broadcasted_iota(jnp.int32, (lanes, chunk), 1)
        start = head * head_dim
        pick = jnp.where((lane >= start) & (lane < start + head_dim), 1.0, 0.0).astype(bf16)
        pick = jnp.concatenate([pick, pick], axis=0)
        return jnp.dot(src[...], pick, preferred_element_type=f32)

    def gather_state(k, _):
        @pl.when(lax.rem(k, group_chunks) == 0)
        def _():
            ready(k // group_chunks)

        cols = pl.ds(pl.multiple_of(k * chunk, chunk), chunk)
        x_conv = conv(x, ex, kx, cols).astype(bf16)
        xc[:, cols] = x_conv
        eld[:, cols] = spread(cat, k)
        weighted = (x_conv.astype(f32) * spread(tocat, k)).astype(bf16)
        total = jnp.dot(bt[k // group_chunks], weighted, preferred_element_type=f32)
        sums[:, cols] = total

        @pl.when(first)
        def _():
            for i in range(pieces):
                outbox[k, i] = total[:, i * piece : (i + 1) * piece].astype(bf16)
                hand_on(k, i).start()

        return 0

    lax.fori_loop(0, chunks, gather_state, 0)
    for load in loads[early:]:
        load.wait()
    for g in range(groups):
        cols = slice(g * state, (g + 1) * state)
        cc[:, cols] = conv(c, ec, kc, cols).astype(bf16)
        scores = jnp.dot(cc[:, cols], bt[g], preferred_element_type=f32)
        sc[g] = jnp.where(causal, scores, 0.0)
    per_tile = lanes // head_dim

    def finish(k, _):
        cols = pl.ds(pl.multiple_of(k * chunk, chunk), chunk)
        g = k // group_chunks
        scores = sc[g]
        columns_of = ldcol[k]
        for j in range(chunk // lanes):
            tile = pl.ds(pl.multiple_of(k * chunk + j * lanes, lanes), lanes)
            x_tile = xc[:, tile]
            lane = lax.broadcasted_iota(jnp.int32, (length, lanes), 1)
            inside = None
            for i in range(per_tile):
                n = j * per_tile + i
                h = k * per_chunk + n
                gap = columns_of[:, n : n + 1] - ldrow[pl.ds(h, 1), :]
                damping = jnp.exp(jnp.minimum(gap, 0.0))
                weights = (damping * steprow[pl.ds(h, 1), :] * scores).astype(bf16)
                term = jnp.dot(weights, x_tile, preferred_element_type=f32)
                inside = term if i == 0 else jnp.where(lane >= i * head_dim, term, inside)
            acc[:, tile] = inside

        @pl.when(me > 0)
        def _():
            for i in range(pieces):
                hand_on(k, i).wait_recv()
                some = pl.ds(pl.multiple_of(k * chunk + i * piece, piece), piece)

                @pl.when(jnp.logical_not(last))
                def _():
                    old = eld[length - 1 : length, some] * inbox[k, i].astype(f32)
                    outbox[k, i] = (old + sums[:, some]).astype(bf16)
                    hand_on(k, i).start()

            c_group = cc[:, pl.ds(pl.multiple_of(g * state, state), state)]
            for i in range(pieces):
                some = pl.ds(pl.multiple_of(k * chunk + i * piece, piece), piece)
                outside = jnp.dot(c_group, inbox[k, i], preferred_element_type=f32)
                acc[:, some] = acc[:, some] + outside * eld[:length, some]

        z_here = z[:, cols].astype(f32)
        total = acc[:, cols] + eld[length : length + 1, cols] * xc[:, cols].astype(f32)
        gated = total * (z_here * jax.nn.sigmoid(z_here))
        acc[:, cols] = gated
        square = gated * gated
        part = square[:, :lanes]
        for j in range(1, chunk // lanes):
            part = part + square[:, j * lanes : (j + 1) * lanes]
        ssq[...] = jnp.where(lax.rem(k, group_chunks) == 0, part, ssq[...] + part)

        @pl.when(lax.rem(k, group_chunks) == group_chunks - 1)
        def _():
            mean = jnp.sum(ssq[...], axis=1, keepdims=True) / (group_chunks * chunk)
            scale = lax.rsqrt(mean + epsilon)
            for j in range(group_chunks):
                first_col = (k - group_chunks + 1 + j) * chunk
                here = pl.ds(pl.multiple_of(first_col, chunk), chunk)
                value = (acc[:, here] * scale * gain[:, here]).astype(bf16)
                for e in range(heads):
                    for q in range(halves):
                        row = (e * halves + q) * rows
                        got[me * halves + q, e * rows : (e + 1) * rows, here] = value[row : row + rows]

        return 0

    lax.fori_loop(0, chunks, finish, 0)

    def gather(shard, peer, q):
        v = shard * halves + q
        return pltpu.make_async_remote_copy(
            got.at[v], got.at[v], ag_send.at[peer * halves + q], ag_recv.at[v],
            device_id={"seq": peer},
        )

    def send_up(v, e):
        return pltpu.make_async_remote_copy(
            part.at[v, e], up.at[v, e], u_send.at[v, e], u_recv.at[v, e],
            device_id={"head": h_z + 1},
        )

    def send_down(v, e):
        return pltpu.make_async_remote_copy(
            part.at[v, e], down.at[v, e], d_send.at[v, e], d_recv.at[v, e],
            device_id={"head": h_z - 1},
        )

    def deliver(peer, source, q):
        rows_out = pl.ds(pl.multiple_of(q * rows, rows), rows)
        columns = pl.ds(pl.multiple_of(source * width, width), width)
        return pltpu.make_async_remote_copy(
            part.at[peer * halves + q, h_z], out.at[rows_out, columns],
            o_send.at[peer * halves + q], o_recv.at[source * halves + q],
            device_id={"section": other, "seq": peer},
        )

    for d in range(1, shards):
        for q in range(halves):
            gather(me, partner(me, d, shards), q).start()

    def multiply(v):
        def one(i, _):
            cols = pl.ds(pl.multiple_of(i * tile, tile), tile)
            terms = jnp.dot(got[v], w_buf[:, cols], preferred_element_type=f32)
            part[v, :, :, cols] = terms.astype(bf16).reshape(heads, rows, tile)
            return 0

        lax.fori_loop(0, tiles, one, 0)

    steps = units * heads

    def decode(t):
        t = jnp.where(t < 0, 0, jnp.where(t < steps, t, steps - 1))
        d, r = t // (heads * halves), t % (heads * halves)
        return partner(me, d, shards), r % halves, r // halves

    def slot(t, _):
        shard, q, k = decode(t)

        @pl.when((t < steps) & (k == 0))
        def _():
            @pl.when(shard != me)
            def _():
                gather(shard, shard, q).wait_recv()

            multiply(shard * halves + q)

        t_up = t - h_z * lag
        shard_u, q_u, k_u = decode(t_up)

        @pl.when((t_up >= 0) & (t_up < steps))
        def _():
            v = shard_u * halves + q_u
            e = end - k_u

            @pl.when((e >= h_z) & (h_z > 0))
            def _():
                send_up(v, e).wait_recv()

            @pl.when((e > h_z) & (h_z > 0))
            def _():
                part[v, e] = (part[v, e].astype(f32) + up[v, e].astype(f32)).astype(bf16)

            @pl.when(e > h_z)
            def _():
                send_up(v, e).start()

        t_down = t - (end - h_z) * lag
        shard_d, q_d, k_d = decode(t_down)

        @pl.when((t_down >= 0) & (t_down < steps))
        def _():
            v = shard_d * halves + q_d

            @pl.when((k_d <= h_z) & (h_z < end))
            def _():
                send_down(v, k_d).wait_recv()

            @pl.when((k_d < h_z) & (h_z < end))
            def _():
                part[v, k_d] = (part[v, k_d].astype(f32) + down[v, k_d].astype(f32)).astype(bf16)

            @pl.when(k_d < h_z)
            def _():
                send_down(v, k_d).start()

        far = jnp.where(2 * h_z > end, h_z, end - h_z)
        t_last = t - far * lag
        shard_l, q_l, k_l = decode(t_last)

        @pl.when((t_last >= 0) & (t_last < steps) & (k_l == far))
        def _():
            v = shard_l * halves + q_l

            @pl.when(h_z == 0)
            def _():
                part[v, h_z] = (part[v, h_z].astype(f32) + down[v, h_z].astype(f32)).astype(bf16)

            @pl.when(h_z == end)
            def _():
                part[v, h_z] = (part[v, h_z].astype(f32) + up[v, h_z].astype(f32)).astype(bf16)

            @pl.when((h_z > 0) & (h_z < end))
            def _():
                total = part[v, h_z].astype(f32) + up[v, h_z].astype(f32)
                part[v, h_z] = (total + down[v, h_z].astype(f32)).astype(bf16)

            deliver(shard_l, here_s, q_l).start()

        return 0

    for load in w_loads:
        load.wait()
    lax.fori_loop(0, steps + end * lag, slot, 0)

    def drain(v, _):
        shard, q = v // halves, v % halves

        @pl.when(shard != me)
        def _():
            gather(me, shard, q).wait_send()

        for e in range(heads):

            @pl.when(e > h_z)
            def _():
                send_up(v, e).wait_send()

            @pl.when(e < h_z)
            def _():
                send_down(v, e).wait_send()

        deliver(shard, here_s, q).wait_send()
        deliver(here_s, shard, q).wait_recv()
        return 0

    lax.fori_loop(0, units, drain, 0)

    @pl.when(jnp.logical_not(last))
    def _():
        for copy in edges:
            copy.wait_send()

        def drain(k, _):
            for i in range(pieces):
                hand_on(k, i).wait_send()
            return 0

        lax.fori_loop(0, chunks, drain, 0)


def layer(args, weight, sizes):
    x, b, c, z, dt, kx, kb, kc, a, bias, skip, gain = args
    sections, shards, heads = sizes
    length, inner = x.shape
    depth, width = weight.shape
    head_count = dt.shape[0]
    head_dim = inner // head_count
    groups = b.shape[1] // N
    chunk, lanes, edge, halves, lag = 256, 128, 8, 2, 3
    chunks = inner // chunk
    count, units = length // halves, halves * shards
    rows = count // heads
    tile = min(512, width)
    f32, bf16 = jnp.float32, jnp.bfloat16
    dma = pltpu.SemaphoreType.DMA
    vmem = pltpu.VMEM
    return pl.pallas_call(
        functools.partial(layer_kernel, sizes, (head_dim, chunk, halves, lag)),
        out_shape=jax.ShapeDtypeStruct((halves * rows, shards * width), bf16),
        in_specs=[pl.BlockSpec(memory_space=pl.ANY)] * 13,
        out_specs=pl.BlockSpec(memory_space=pl.ANY),
        scratch_shapes=[vmem(array.shape, array.dtype) for array in args]
        + [
            dma((12,)),
            vmem((edge, inner), bf16),
            vmem((edge, b.shape[1]), bf16),
            vmem((edge, b.shape[1]), bf16),
            vmem((edge + length, chunk), f32),
            vmem((length, inner), bf16),
            vmem((groups, N, length), bf16),
            vmem((length, groups * N), bf16),
            vmem((groups, length, length), f32),
            vmem((24, lanes), f32),
            vmem((lanes, length), f32),
            vmem((lanes, length), f32),
            vmem((lanes, length), f32),
            vmem((chunks, length, chunk // head_dim), f32),
            vmem((length + 16, 2 * lanes), bf16),
            vmem((length, 2 * lanes), bf16),
            vmem((length + 16, inner), f32),
            vmem((N, inner), f32),
            vmem((length, inner), f32),
            vmem((length, lanes), f32),
            vmem((chunks, chunk // lanes, N, lanes), bf16),
            vmem((chunks, chunk // lanes, N, lanes), bf16),
            dma((3,)),
            dma((3,)),
            dma((chunks, chunk // lanes)),
            dma((chunks, chunk // lanes)),
            vmem(weight.shape, bf16),
            vmem((units, count, depth), bf16),
            vmem((units, heads, rows, width), bf16),
            vmem((units, heads, rows, width), bf16),
            vmem((units, heads, rows, width), bf16),
            dma((width // tile,)),
            dma((units,)),
            dma((units,)),
            dma((units, heads)),
            dma((units, heads)),
            dma((units, heads)),
            dma((units, heads)),
            dma((units,)),
            dma((units,)),
        ],
        compiler_params=pltpu.CompilerParams(
            collective_id=0, has_side_effects=True, vmem_limit_bytes=63 * 2**20
        ),
        cost_estimate=pl.CostEstimate(
            flops=2 * length * shards * depth * width,
            bytes_accessed=2 * weight.size,
            transcendentals=0,
        ),
        name="layer",
    )(*args, weight)


def per_device(
    x_in,
    b_in,
    c_in,
    z_in,
    dt_raw,
    conv_x,
    conv_b,
    conv_c,
    a_rate,
    dt_bias,
    skip_d,
    norm_gain,
    out_weight,
):
    sizes = tuple(lax.axis_size(name) for name in ("section", "seq", "head"))
    whole = (x_in, b_in, c_in, z_in, dt_raw, conv_x, conv_b, conv_c)
    args = [array[0] for array in whole] + [a_rate, dt_bias, skip_d, norm_gain]
    return layer(args, out_weight[0], sizes)[None]


def solution(mesh):
    return jax.shard_map(
        per_device,
        mesh=mesh,
        in_specs=(
            P("section", "seq", "head"),
            P("section", "seq", "head"),
            P("section", "seq", "head"),
            P("section", "seq", "head"),
            P("section", "head", "seq"),
            P("section", None, "head"),
            P("section", None, "head"),
            P("section", None, "head"),
            P("section", "head"),
            P("section", "head"),
            P("section", "head"),
            P("section", "head"),
            P("section", "head", "seq"),
        ),
        out_specs=P("section", ("seq", "head"), None),
        check_vma=False,
    )
```

time: 130 us -> 126 us (0.969); the launches traced: 128 us -> 126 us
  local copies, waits for them, and re-layouts: 3.63 us -> 2.26 us
    reshape x1 -> x0, local copies, waits for them, and re-layouts: 1.6 us -> none  [per_device(): return jnp.transpose(mixed, (0, 2, 1, 3)).reshape(1, halves * rows, -1)]
    pallas_call x2 -> x1, Pallas kernels: 125 us -> 124 us  [layer(): pl.pallas_call(functools.partial(layer_kernel, sizes, (head_dim, chunk, h...]
where the time goes in v2:
time: 126 us
  Pallas kernels  124 us (98%)
  local copies, waits for them, and re-layouts  2.26 us (2%)
    pallas_call x1, Pallas kernels, layer(): pl.pallas_call(functools.partial(layer_kernel, sizes, (head_dim, chunk, h...  124 us

profile of v2, /device:TPU:1, one launch (start us, length us, event | category | flops | bytes accessed | tf_op | source)
XLA Modules:
  0.0 126.1 jit_solution(3954350110833215103)
XLA Ops:
  0.0 123.9 %layer.1 = bf16[64,8192]{1,0:T(8,128)(2,1)} custom-call(bf16[256,2048]{1,0:T(8,128)(2,1)} %bitcast.12, bf16[256,512]{1,0:T(8,128)(2,1)} %bitcast.14, bf16[256,512]{1,0:T(8,128)(2,1)} %bitcast.15, bf16[256,2048]{1,0:T(8,128)(2,1)} %bitcast.13, f32[32,256]{1,0:T(8,128)} %bitcast.16, f32[4,2048]{1,0:T(4,128)} %bitcast.17, f32[4,512]{1,0:T(4,128)} %bitcast.18, ...), custom_call_target="tpu_custom_call" | custom-call | flops 8589934592 | bytes 8388608 | tf_op jit(solution)/shard_map/layer/pallas_call | solution.py:458
  123.9 2.3 %copy.15 = bf16[1,64,8192]{2,1,0:T(8,128)(2,1)} copy(bf16[1,64,8192]{2,1,0:T(8,128)(2,1)} %bitcast.10) | data formatting | bytes 2097152

commit v3 on v2

--- a/solution.py
+++ b/solution.py
@@ -26,7 +26,7 @@
     sizes, dims, x_hbm, b_hbm, c_hbm, z_hbm, dt_hbm, kx_hbm, kb_hbm, kc_hbm, a_hbm, bias_hbm,
     skip_hbm, gain_hbm, weight, out, x, b, c, z, dt, kx, kb, kc, a, bias, skip, gain, loaded,
     ex, eb, ec, pad, xc, bt, cc, sc, vec, dtp, ldrow, steprow, ldcol, cat, tocat,
-    eld, sums, acc, ssq, inbox, outbox, e_send, e_recv, send, recv,
+    eld, sums, acc, gate, keep, ssq, inbox, outbox, e_send, e_recv, send, recv,
     w_buf, got, part, up, down,
     w_sem, ag_send, ag_recv, u_send, u_recv, d_send, d_recv, o_send, o_recv,
 ):
@@ -96,12 +96,13 @@
         for n, (src, dst) in enumerate(((x_hbm, ex), (b_hbm, eb), (c_hbm, ec)))
     ]
 
-    pieces = outbox.shape[1]
-    piece = outbox.shape[3]
-
-    def hand_on(k, i):
+    pieces, slices = outbox.shape[1:3]
+    piece = outbox.shape[4]
+    deep = state // slices
+
+    def hand_on(k, i, j):
         return pltpu.make_async_remote_copy(
-            outbox.at[k, i], inbox.at[k, i], send.at[k, i], recv.at[k, i],
+            outbox.at[k, i, j], inbox.at[k, i, j], send.at[k, i, j], recv.at[k, i, j],
             device_id={"seq": after},
         )
 
@@ -134,10 +135,8 @@
         high = rest.astype(bf16)
         decay = decay + jnp.dot(below, high, preferred_element_type=f32)
         rest = rest - high.astype(f32)
-    ldrow[...] = decay.T
-    steprow[...] = step.T
-    for k in range(chunks):
-        ldcol[k] = decay[:, k * per_chunk : (k + 1) * per_chunk]
+    keep[0] = decay
+    keep[1] = step
 
     def split(dst, value, first_row):
         size = value.shape[0]
@@ -145,8 +144,6 @@
         dst[first_row : first_row + size, :lanes] = high
         dst[first_row : first_row + size, lanes:] = (value - high.astype(f32)).astype(bf16)
 
-    split(cat, jnp.exp(decay), 0)
-    split(cat, jnp.broadcast_to(vec[16:17, :], (16, lanes)), length)
     split(tocat, jnp.exp(decay[length - 1 : length, :] - decay) * step, 0)
 
     for load in loads[small:early]:
@@ -188,7 +185,6 @@
         cols = pl.ds(pl.multiple_of(k * chunk, chunk), chunk)
         x_conv = conv(x, ex, kx, cols).astype(bf16)
         xc[:, cols] = x_conv
-        eld[:, cols] = spread(cat, k)
         weighted = (x_conv.astype(f32) * spread(tocat, k)).astype(bf16)
         total = jnp.dot(bt[k // group_chunks], weighted, preferred_element_type=f32)
         sums[:, cols] = total
@@ -196,14 +192,23 @@
         @pl.when(first)
         def _():
             for i in range(pieces):
-                outbox[k, i] = total[:, i * piece : (i + 1) * piece].astype(bf16)
-                hand_on(k, i).start()
+                for j in range(slices):
+                    some = total[j * deep : (j + 1) * deep, i * piece : (i + 1) * piece]
+                    outbox[k, i, j] = some.astype(bf16)
+                    hand_on(k, i, j).start()
 
         return 0
 
     lax.fori_loop(0, chunks, gather_state, 0)
     for load in loads[early:]:
         load.wait()
+    decay = keep[0]
+    ldrow[...] = decay.T
+    steprow[...] = keep[1].T
+    for k in range(chunks):
+        ldcol[k] = decay[:, k * per_chunk : (k + 1) * per_chunk]
+    split(cat, jnp.exp(decay), 0)
+    split(cat, jnp.broadcast_to(vec[16:17, :], (16, lanes)), length)
     for g in range(groups):
         cols = slice(g * state, (g + 1) * state)
         cc[:, cols] = conv(c, ec, kc, cols).astype(bf16)
@@ -214,6 +219,9 @@
     def finish(k, _):
         cols = pl.ds(pl.multiple_of(k * chunk, chunk), chunk)
         g = k // group_chunks
+        eld[:, cols] = spread(cat, k)
+        z_here = z[:, cols].astype(f32)
+        gate[...] = z_here * jax.nn.sigmoid(z_here)
         scores = sc[g]
         columns_of = ldcol[k]
         for j in range(chunk // lanes):
@@ -229,29 +237,30 @@
                 weights = (damping * steprow[pl.ds(h, 1), :] * scores).astype(bf16)
                 term = jnp.dot(weights, x_tile, preferred_element_type=f32)
                 inside = term if i == 0 else jnp.where(lane >= i * head_dim, term, inside)
-            acc[:, tile] = inside
+            acc[:, tile] = inside + eld[length : length + 1, tile] * x_tile.astype(f32)
 
         @pl.when(me > 0)
         def _():
             for i in range(pieces):
-                hand_on(k, i).wait_recv()
                 some = pl.ds(pl.multiple_of(k * chunk + i * piece, piece), piece)
-
-                @pl.when(jnp.logical_not(last))
-                def _():
-                    old = eld[length - 1 : length, some] * inbox[k, i].astype(f32)
-                    outbox[k, i] = (old + sums[:, some]).astype(bf16)
-                    hand_on(k, i).start()
+                for j in range(slices):
+                    hand_on(k, i, j).wait_recv()
+
+                    @pl.when(jnp.logical_not(last))
+                    def _():
+                        old = eld[length - 1 : length, some] * inbox[k, i, j].astype(f32)
+                        new = old + sums[j * deep : (j + 1) * deep, some]
+                        outbox[k, i, j] = new.astype(bf16)
+                        hand_on(k, i, j).start()
 
             c_group = cc[:, pl.ds(pl.multiple_of(g * state, state), state)]
             for i in range(pieces):
                 some = pl.ds(pl.multiple_of(k * chunk + i * piece, piece), piece)
-                outside = jnp.dot(c_group, inbox[k, i], preferred_element_type=f32)
+                here = inbox[k, i].reshape(state, piece)
+                outside = jnp.dot(c_group, here, preferred_element_type=f32)
                 acc[:, some] = acc[:, some] + outside * eld[:length, some]
 
-        z_here = z[:, cols].astype(f32)
-        total = acc[:, cols] + eld[length : length + 1, cols] * xc[:, cols].astype(f32)
-        gated = total * (z_here * jax.nn.sigmoid(z_here))
+        gated = acc[:, cols] * gate[...]
         acc[:, cols] = gated
         square = gated * gated
         part = square[:, :lanes]
@@ -304,9 +313,12 @@
             device_id={"section": other, "seq": peer},
         )
 
-    for d in range(1, shards):
-        for q in range(halves):
-            gather(me, partner(me, d, shards), q).start()
+    def spread_rows(distances):
+        for d in distances:
+            for q in range(halves):
+                gather(me, partner(me, d, shards), q).start()
+
+    spread_rows(range(1, min(3, shards)))
 
     def multiply(v):
         def one(i, _):
@@ -325,6 +337,10 @@
         return partner(me, d, shards), r % halves, r // halves
 
     def slot(t, _):
+        @pl.when(t == 2 * heads * halves)
+        def _():
+            spread_rows(range(3, shards))
+
         shard, q, k = decode(t)
 
         @pl.when((t < steps) & (k == 0))
@@ -433,7 +449,8 @@
 
         def drain(k, _):
             for i in range(pieces):
-                hand_on(k, i).wait_send()
+                for j in range(slices):
+                    hand_on(k, i, j).wait_send()
             return 0
 
         lax.fori_loop(0, chunks, drain, 0)
@@ -448,7 +465,7 @@
     head_dim = inner // head_count
     groups = b.shape[1] // N
     chunk, lanes, edge, halves, lag = 256, 128, 8, 2, 3
-    chunks = inner // chunk
+    chunks, slices = inner // chunk, 1
     count, units = length // halves, halves * shards
     rows = count // heads
     tile = min(512, width)
@@ -481,13 +498,15 @@
             vmem((length + 16, inner), f32),
             vmem((N, inner), f32),
             vmem((length, inner), f32),
+            vmem((length, chunk), f32),
+            vmem((2, length, lanes), f32),
             vmem((length, lanes), f32),
-            vmem((chunks, chunk // lanes, N, lanes), bf16),
-            vmem((chunks, chunk // lanes, N, lanes), bf16),
+            vmem((chunks, chunk // lanes, slices, N // slices, lanes), bf16),
+            vmem((chunks, chunk // lanes, slices, N // slices, lanes), bf16),
             dma((3,)),
             dma((3,)),
-            dma((chunks, chunk // lanes)),
-            dma((chunks, chunk // lanes)),
+            dma((chunks, chunk // lanes, slices)),
+            dma((chunks, chunk // lanes, slices)),
             vmem(weight.shape, bf16),
             vmem((units, count, depth), bf16),
             vmem((units, heads, rows, width), bf16),

time: 126 us -> 125 us (level)
  no operation moved by 1% of the time
where the time goes in v3:
time: 125 us
  Pallas kernels  123 us (98%)
  local copies, waits for them, and re-layouts  2.26 us (2%)
    pallas_call x1, Pallas kernels, layer(): pl.pallas_call(functools.partial(layer_kernel, sizes, (head_dim, chunk, h...  123 us

profile of v3, /device:TPU:1, one launch (start us, length us, event | category | flops | bytes accessed | tf_op | source)
XLA Modules:
  0.0 124.9 jit_solution(2333031974294715297)
XLA Ops:
  0.0 122.6 %layer.1 = bf16[64,8192]{1,0:T(8,128)(2,1)} custom-call(bf16[256,2048]{1,0:T(8,128)(2,1)} %bitcast.12, bf16[256,512]{1,0:T(8,128)(2,1)} %bitcast.14, bf16[256,512]{1,0:T(8,128)(2,1)} %bitcast.15, bf16[256,2048]{1,0:T(8,128)(2,1)} %bitcast.13, f32[32,256]{1,0:T(8,128)} %bitcast.16, f32[4,2048]{1,0:T(4,128)} %bitcast.17, f32[4,512]{1,0:T(4,128)} %bitcast.18, ...), custom_call_target="tpu_custom_call" | custom-call | flops 8589934592 | bytes 8388608 | tf_op jit(solution)/shard_map/layer/pallas_call | solution.py:475
  122.6 2.3 %copy.15 = bf16[1,64,8192]{2,1,0:T(8,128)(2,1)} copy(bf16[1,64,8192]{2,1,0:T(8,128)(2,1)} %bitcast.10) | data formatting | bytes 2097152

commit v4 on v3

--- a/solution.py
+++ b/solution.py
@@ -35,7 +35,7 @@
     count = got.shape[1]
     units = shards * halves
     rows, width = part.shape[2], part.shape[3]
-    tile = min(512, width)
+    tile = min(1024, width)
     tiles = width // tile
     f32, bf16 = jnp.float32, jnp.bfloat16
     here_s, h_z = lax.axis_index("seq"), lax.axis_index("head")
@@ -468,7 +468,7 @@
     chunks, slices = inner // chunk, 1
     count, units = length // halves, halves * shards
     rows = count // heads
-    tile = min(512, width)
+    tile = min(1024, width)
     f32, bf16 = jnp.float32, jnp.bfloat16
     dma = pltpu.SemaphoreType.DMA
     vmem = pltpu.VMEM

time: 125 us -> 125 us (level)
  no operation moved by 1% of the time
where the time goes in v4:
time: 125 us
  Pallas kernels  122 us (98%)
  local copies, waits for them, and re-layouts  2.26 us (2%)
    pallas_call x1, Pallas kernels, layer(): pl.pallas_call(functools.partial(layer_kernel, sizes, (head_dim, chunk, h...  122 us

profile of v4, /device:TPU:1, one launch (start us, length us, event | category | flops | bytes accessed | tf_op | source)
XLA Modules:
  0.0 124.5 jit_solution(16485135168117177401)
XLA Ops:
  0.0 122.2 %layer.1 = bf16[64,8192]{1,0:T(8,128)(2,1)} custom-call(bf16[256,2048]{1,0:T(8,128)(2,1)} %bitcast.12, bf16[256,512]{1,0:T(8,128)(2,1)} %bitcast.14, bf16[256,512]{1,0:T(8,128)(2,1)} %bitcast.15, bf16[256,2048]{1,0:T(8,128)(2,1)} %bitcast.13, f32[32,256]{1,0:T(8,128)} %bitcast.16, f32[4,2048]{1,0:T(4,128)} %bitcast.17, f32[4,512]{1,0:T(4,128)} %bitcast.18, ...), custom_call_target="tpu_custom_call" | custom-call | flops 8589934592 | bytes 8388608 | tf_op jit(solution)/shard_map/layer/pallas_call | solution.py:475
  122.2 2.3 %copy.15 = bf16[1,64,8192]{2,1,0:T(8,128)(2,1)} copy(bf16[1,64,8192]{2,1,0:T(8,128)(2,1)} %bitcast.10) | data formatting | bytes 2097152
